TPU v7x, 32 devices: a whole 2x2x4 slice. The times are simulated.
32 devices in a mesh: rep: 16 (over z, y, x), dom: 2 (over core).
Axes of the slice: x: 2, y: 2, z: 4, core: 2. Of those that a mesh axis runs over, the one named last changes fastest.
Arguments:
- protein_pos: float32 [3, 65536], P(None, ('rep', 'dom')), parts along dimension 1, may hold values from -4 to 4, as said below
- protein_vel: float32 [3, 65536], P(None, ('rep', 'dom')), parts along dimension 1, may hold values from -3 to 3
- inv_mass: float32 [65536], P(('rep', 'dom')), parts along dimension 0, may hold values from 0.0625 to 1
- bond_atoms: int32 [2, 40960], P(None, ('rep', 'dom')), parts along dimension 1, may hold values from 0 to 2047, as said below
- left_atoms: int32 [12288], P(('rep', 'dom')), parts along dimension 0, may hold values from 0 to 2047, as said below
- right_atoms: int32 [12288], P(('rep', 'dom')), parts along dimension 0, may hold values from 0 to 2047, as said below
- water_pos: float32 [9, 32768], P(None, ('rep', 'dom')), parts along dimension 1, may hold values from -3.2 to 3.2, as said below
- water_vel: float32 [9, 32768], P(None, ('rep', 'dom')), parts along dimension 1, may hold values from -3 to 3
Outputs:
- protein_velocity: float32 [3, 65536], P(None, ('rep', 'dom')), parts along dimension 1
- water_velocity: float32 [9, 32768], P(None, ('rep', 'dom')), parts along dimension 1
There are 16 independent parts, one for each index of `rep`. A program takes and returns all parts, laid end to end along the dimension named above; each array names one. Nothing has to cross between parts.
Inputs may be any that keep to these rules, and one draw needn't show every extreme that they name: `bond_atoms`: indices within the domain's block of 2048 atoms; each column joins two different atoms; together with the cross bonds the bonds form a forest. `left_atoms`: distinct indices within the domain's block, none of them in right_atoms. `right_atoms`: distinct indices within the domain's block. `protein_pos`: every bond and every cross bond joins atoms 0.1 to 0.15 apart. `water_pos`: each column holds one rigid water: oxygen, then two hydrogens, 0.09572 from the oxygen and 0.15139 from each other.
All inputs are finite; a program needn't handle non-finite values.
Results may differ from a plain program's by a relative error of at most 0.0003.
Values sent between devices are 32-bit elements; how exact they have to be, the bound alone decides.
A program may use at most 64 MiB of HBM per device.

v0:
```python
import functools
import math

import jax
import jax.numpy as jnp
from jax import lax
from jax.experimental import pallas as pl
from jax.experimental.pallas import tpu as pltpu
from jax.sharding import PartitionSpec as P

ORDER = 4
ITER = 2
LANES = 128
SUB = 8


time_step = 0.002
mass_oxygen = 15.9994
mass_hydrogen = 1.008
oxygen_hydrogen = 0.09572
hydrogen_pair = 0.15139
total_mass = mass_oxygen + 2.0 * mass_hydrogen
half_pair = 0.5 * hydrogen_pair
water_height = math.sqrt(oxygen_hydrogen * oxygen_hydrogen - half_pair * half_pair)
oxygen_reach = 2.0 * mass_hydrogen * water_height / total_mass
hydrogen_reach = water_height - oxygen_reach


def cross_product(left, right):
    return [
        left[1] * right[2] - left[2] * right[1],
        left[2] * right[0] - left[0] * right[2],
        left[0] * right[1] - left[1] * right[0],
    ]


def inner(left, right):
    return left[0] * right[0] + left[1] * right[1] + left[2] * right[2]


def minus(left, right):
    return [a - b for a, b in zip(left, right)]


def settle(before, after):
    old_oxygen, old_first, old_second = (before[0:3], before[3:6], before[6:9])
    new_oxygen, new_first, new_second = (after[0:3], after[3:6], after[6:9])
    center = [
        (mass_oxygen * o + mass_hydrogen * (f + s)) / total_mass
        for o, f, s in zip(new_oxygen, new_first, new_second)
    ]
    old_b = minus(old_first, old_oxygen)
    old_c = minus(old_second, old_oxygen)
    rel_a = minus(new_oxygen, center)
    rel_b = minus(new_first, center)
    rel_c = minus(new_second, center)
    normal = cross_product(old_b, old_c)
    side = cross_product(rel_a, normal)
    upward = cross_product(normal, side)

    def normed(vector):
        size = jnp.sqrt(inner(vector, vector))
        return [a / size for a in vector]

    axis_z = normed(normal)
    axis_x = normed(side)
    axis_y = normed(upward)
    oldb_x = inner(axis_x, old_b)
    oldb_y = inner(axis_y, old_b)
    oldc_x = inner(axis_x, old_c)
    oldc_y = inner(axis_y, old_c)
    newa_z = inner(axis_z, rel_a)
    newb_x = inner(axis_x, rel_b)
    newb_y = inner(axis_y, rel_b)
    newb_z = inner(axis_z, rel_b)
    newc_x = inner(axis_x, rel_c)
    newc_y = inner(axis_y, rel_c)
    newc_z = inner(axis_z, rel_c)
    sin_phi = newa_z / oxygen_reach
    cos_phi = jnp.sqrt(1.0 - sin_phi * sin_phi)
    sin_psi = (newb_z - newc_z) / (2.0 * half_pair * cos_phi)
    cos_psi = jnp.sqrt(1.0 - sin_psi * sin_psi)
    rest_ay = oxygen_reach * cos_phi
    rest_bx = -half_pair * cos_psi
    lowered = -hydrogen_reach * cos_phi
    tilted = half_pair * sin_psi * sin_phi
    rest_by = lowered - tilted
    rest_cy = lowered + tilted
    alpha = rest_bx * (oldb_x - oldc_x) + oldb_y * rest_by + oldc_y * rest_cy
    beta = rest_bx * (oldc_y - oldb_y) + oldb_x * rest_by + oldc_x * rest_cy
    gamma = oldb_x * newb_y - newb_x * oldb_y + oldc_x * newc_y - newc_x * oldc_y
    summed = alpha * alpha + beta * beta
    sin_theta = (alpha * gamma - beta * jnp.sqrt(summed - gamma * gamma)) / summed
    cos_theta = jnp.sqrt(1.0 - sin_theta * sin_theta)
    final_ax = -rest_ay * sin_theta
    final_ay = rest_ay * cos_theta
    final_bx = rest_bx * cos_theta - rest_by * sin_theta
    final_by = rest_bx * sin_theta + rest_by * cos_theta
    final_cx = -rest_bx * cos_theta - rest_cy * sin_theta
    final_cy = -rest_bx * sin_theta + rest_cy * cos_theta

    def placed(x, y, z):
        return [
            center[c] + axis_x[c] * x + axis_y[c] * y + axis_z[c] * z for c in range(3)
        ]

    return (
        placed(final_ax, final_ay, newa_z)
        + placed(final_bx, final_by, newb_z)
        + placed(final_cx, final_cy, newc_z)
    )


def lane_gather(table, index):
    return jnp.take_along_axis(table, index, axis=1, mode="promise_in_bounds")


def kernel(
    n, axis, pos, vel, mass, bonds, left, right, wpos, wvel, out_p, out_w,
    pos_x, vel_x, mass_x, bonds_x, left_x, right_x,
    first_s, second_s, packed_s, rows_s, lanes_s, lhs_s, field_s, water_s,
    send_sem, recv_sem,
):
    atom_rows = mass.shape[0]
    bond_rows = bonds.shape[1] // LANES
    halo_rows = left.shape[0]
    used = bond_rows + halo_rows
    con_rows = first_s.shape[1]
    tiles = con_rows // SUB
    half_rows = 2 * used
    water_rows = wpos.shape[1] // LANES

    own = (pos, vel, mass, bonds, left, right)
    others = (pos_x, vel_x, mass_x, bonds_x, left_x, right_x)
    me = lax.axis_index(axis)
    copies = []
    if n > 1:
        barrier = pltpu.get_barrier_semaphore()
        for k in range(1, n):
            peer = lax.rem(me + k, n)
            pl.semaphore_signal(
                barrier, inc=1, device_id={axis: peer},
                device_id_type=pl.DeviceIdType.MESH,
            )
        pl.semaphore_wait(barrier, n - 1)
        for k in range(1, n):
            peer = lax.rem(me + n - k, n)
            for t in range(len(own)):
                copy = pltpu.make_async_remote_copy(
                    src_ref=own[t],
                    dst_ref=others[t].at[k - 1],
                    send_sem=send_sem.at[k - 1, t],
                    recv_sem=recv_sem.at[k - 1, t],
                    device_id={axis: peer},
                    device_id_type=pl.DeviceIdType.MESH,
                )
                copy.start()
                copies.append(copy)

    components = wpos.shape[0]
    for source, base in ((wpos, 0), (wvel, components)):
        for c in range(components):
            for r in range(water_rows):
                water_s[base + c, pl.ds(r, 1), :] = source[
                    pl.ds(c, 1), pl.ds(r * LANES, LANES)
                ]
    before = [water_s[c] for c in range(components)]
    speed = [water_s[components + c] for c in range(components)]
    after = [b + time_step * v for b, v in zip(before, speed)]
    settled = settle(before, after)
    for c in range(components):
        water_s[c] = speed[c] + (settled[c] - after[c]) / time_step
    for c in range(components):
        for r in range(water_rows):
            out_w[pl.ds(c, 1), pl.ds(r * LANES, LANES)] = water_s[c, pl.ds(r, 1), :]

    def data(k):
        return own if k == 0 else tuple(ref.at[k - 1] for ref in others)

    def index_bonds(k):
        bonds_k = data(k)[3]
        for r in range(bond_rows):
            first_s[k, pl.ds(r, 1), :] = bonds_k[pl.ds(0, 1), pl.ds(r * LANES, LANES)]
            second_s[k, pl.ds(r, 1), :] = bonds_k[pl.ds(1, 1), pl.ds(r * LANES, LANES)]

    def index_cross(k):
        blank = jnp.zeros((con_rows - used, LANES), jnp.int32)
        first_s[k, pl.ds(used, con_rows - used), :] = blank
        second_s[k, pl.ds(used, con_rows - used), :] = blank
        first_s[k, pl.ds(bond_rows, halo_rows), :] = data(k)[5][...]
        second_s[k, pl.ds(bond_rows, halo_rows), :] = data((k + 1) % n)[4][...]

    row_iota = lax.broadcasted_iota(jnp.int32, (atom_rows, LANES), 0)
    lane_iota = lax.broadcasted_iota(jnp.int32, (LANES, LANES), 0)
    pure = bond_rows // SUB
    half_source, half_index = [], []
    for k in range(n):
        sources = [(k, r, first_s, k, 1.0) for r in range(used)]
        sources += [(k, r, second_s, k, -1.0) for r in range(bond_rows)]
        back = (k + n - 1) % n
        sources += [(back, r, second_s, back, -1.0) for r in range(bond_rows, used)]
        sources.sort(key=lambda item: item[1] >= pure * SUB)
        half_source.append([(s[0], s[1]) for s in sources])
        half_index.append(sources)

    def one_hots(k, chosen):
        for p in chosen:
            _, r, ref, slot, sign = half_index[k][p]
            index = ref[slot, pl.ds(r, 1), :]
            rows_s[k, p] = jnp.where(row_iota == (index >> 7), sign, 0.0).astype(
                jnp.bfloat16
            )
            lanes_s[k, :, pl.ds(p * LANES, LANES)] = jnp.where(
                lane_iota == (index & 127), 1.0, 0.0
            ).astype(jnp.bfloat16)

    position = lax.broadcasted_iota(jnp.int32, (SUB, LANES), 0)
    valid = [position + v * SUB < used for v in range(tiles)]

    def one_end(k, v, ref, tables):
        following = (k + 1) % n
        index = ref[k, pl.ds(v * SUB, SUB), :]
        lane, row = index & 127, index >> 7
        low, high = v * SUB, (v + 1) * SUB
        found = [None] * len(tables)
        for r in range(atom_rows):
            hit = row == r
            for c, table in enumerate(tables):
                source = jnp.broadcast_to(table(k, r), (SUB, LANES))
                if ref is second_s and high > bond_rows:
                    there = jnp.broadcast_to(table(following, r), (SUB, LANES))
                    if low < bond_rows:
                        there = jnp.where(position + low < bond_rows, source, there)
                    source = there
                got = lane_gather(source, lane)
                found[c] = got if r == 0 else jnp.where(hit, got, found[c])
        return found

    unit, length, scale, gap, value = (
        [[None] * tiles for _ in range(n)] for _ in range(5)
    )
    tables = []
    for which in (0, 1):
        for c in range(3):
            tables.append(
                lambda slot, r, which=which, c=c: data(slot)[which][
                    pl.ds(c, 1), pl.ds(r * LANES, LANES)
                ]
            )
    tables.append(lambda slot, r: data(slot)[2][pl.ds(r, 1), :])

    def start(k, v):
        at_i = one_end(k, v, first_s, tables)
        at_j = one_end(k, v, second_s, tables)
        diff = minus(at_i[0:3], at_j[0:3])
        size = jnp.where(valid[v], jnp.sqrt(inner(diff, diff)), 1.0)
        moved_i = [p + time_step * q for p, q in zip(at_i[0:3], at_i[3:6])]
        moved_j = [p + time_step * q for p, q in zip(at_j[0:3], at_j[3:6])]
        unit[k][v] = [d / size for d in diff]
        length[k][v] = size
        scale[k][v] = jnp.where(valid[v], 1.0 / jnp.sqrt(at_i[6] + at_j[6]), 0.0)
        gap[k][v] = minus(moved_i, moved_j)
        value[k][v] = scale[k][v] * (inner(unit[k][v], gap[k][v]) - size)

    early = 2 * pure * SUB
    index_bonds(0)
    one_hots(0, range(early))
    for v in range(pure):
        start(0, v)
    for copy in copies:
        copy.wait()
    for k in range(1, n):
        index_bonds(k)
    for k in range(n):
        index_cross(k)
    one_hots(0, range(early, half_rows))
    for k in range(1, n):
        one_hots(k, range(half_rows))
    for k in range(n):
        for v in range(tiles):
            if k > 0 or v >= pure:
                start(k, v)
    scaled_unit = [
        [[scale[k][v] * u for u in unit[k][v]] for v in range(tiles)] for k in range(n)
    ]

    def pack(values, pairs):
        for k, v in pairs:
            rows = pl.ds(v * SUB, SUB)
            for c in range(3):
                weighted = scaled_unit[k][v][c] * values[k][v]
                high = weighted.astype(jnp.bfloat16).astype(jnp.float32)
                packed_s[k, c, rows, :] = high
                packed_s[k, 3 + c, rows, :] = weighted - high

    cuts = []
    for low, high in ((0, early), (early, half_rows)):
        middle = low + (high - low) // 4 * 2
        cuts += [(a, b) for a, b in ((low, middle), (middle, high)) if b > a]

    def make_field(k):
        summed = None
        for low, high in cuts:
            for p in range(low, high):
                slot, r = half_source[k][p]
                hot = rows_s[k, p]
                for j in range(6):
                    wide = jnp.broadcast_to(
                        packed_s[slot, j, pl.ds(r, 1), :], (atom_rows, LANES)
                    ).astype(jnp.bfloat16)
                    lhs_s[k, pl.ds(j * atom_rows, atom_rows), pl.ds(p * LANES, LANES)] = (
                        wide * hot
                    )
            columns = pl.ds(low * LANES, (high - low) * LANES)
            part = lax.dot_general(
                lhs_s[k, :, columns], lanes_s[k, :, columns], (((1,), (1,)), ((), ())),
                preferred_element_type=jnp.float32,
            )
            summed = part if summed is None else summed + part
        weight = data(k)[2][...]
        for c in range(3):
            field_s[k, c] = weight * (
                summed[c * atom_rows:(c + 1) * atom_rows]
                + summed[(3 + c) * atom_rows:(4 + c) * atom_rows]
            )

    field_tables = [
        lambda slot, r, c=c: field_s[slot, c, pl.ds(r, 1), :] for c in range(3)
    ]
    mine = [(0, v) for v in range(tiles)]
    theirs = [(k, v) for k in range(1, n) for v in range(tiles)]
    order = (
        [(0, v) for v in range(pure)]
        + [(k, v) for k in range(n) for v in range(pure, tiles)]
        + [(k, v) for k in range(1, n) for v in range(pure)]
    )

    def other_fields():
        for k in range(1, n):
            make_field(k)

    def field_gaps():
        gaps = [[None] * tiles for _ in range(n)]
        for k, v in order:
            at_i = one_end(k, v, first_s, field_tables)
            at_j = one_end(k, v, second_s, field_tables)
            gaps[k][v] = minus(at_i, at_j)
        return gaps

    def over(function, *series):
        return [
            [function(*[x[k][v] for x in series]) for v in range(tiles)]
            for k in range(n)
        ]

    def one_order(step, carry):
        current, total = carry
        other_fields()
        current = over(
            lambda x, su, g: x - inner(su, g), current, scaled_unit, field_gaps()
        )
        total = over(lambda t, x: t + x, total, current)
        following = over(lambda x, t: jnp.where(step == ORDER - 1, t, x), current, total)
        pack(following, mine + theirs)
        make_field(0)
        return current, total

    def expand(values):
        pack(values, mine + theirs)
        make_field(0)
        lax.fori_loop(0, ORDER, one_order, (values, values))
        return [field_s[0, c] for c in range(3)]

    def one_round(_, carry):
        gap, value, moved_by = carry
        own_field = expand(value)
        other_fields()
        gap = over(minus, gap, field_gaps())
        value = over(
            lambda s, l, g: s * (l - jnp.sqrt(2.0 * l * l - inner(g, g))),
            scale, length, gap,
        )
        return gap, value, [m + f for m, f in zip(moved_by, own_field)]

    zero = jnp.zeros((atom_rows, LANES), jnp.float32)
    gap, value, moved_by = lax.fori_loop(0, ITER, one_round, (gap, value, [zero] * 3))
    moved_by = [m + f for m, f in zip(moved_by, expand(value))]
    for c in range(3):
        field_s[0, c] = moved_by[c] / time_step
    for c in range(3):
        for r in range(atom_rows):
            cols = pl.ds(r * LANES, LANES)
            out_p[pl.ds(c, 1), cols] = (
                vel[pl.ds(c, 1), cols] - field_s[0, c, pl.ds(r, 1), :]
            )


def on_device(
    n, protein_pos, protein_vel, inv_mass, bond_atoms, left_atoms, right_atoms, water_pos, water_vel
):
    atoms = protein_pos.shape[1]
    atom_rows = atoms // LANES
    bond_rows = bond_atoms.shape[1] // LANES
    halo_rows = left_atoms.shape[0] // LANES
    con_rows = -(-(bond_rows + halo_rows + 1) // SUB) * SUB
    half = 2 * (bond_rows + halo_rows)
    others = max(n - 1, 1)
    mass = inv_mass.reshape(atom_rows, LANES)
    left = left_atoms.reshape(halo_rows, LANES)
    right = right_atoms.reshape(halo_rows, LANES)
    operands = (protein_pos, protein_vel, mass, bond_atoms, left, right, water_pos, water_vel)
    vmem = pl.BlockSpec(memory_space=pltpu.VMEM)
    return pl.pallas_call(
        functools.partial(kernel, n, "dom"),
        out_shape=(
            jax.ShapeDtypeStruct(protein_vel.shape, jnp.float32),
            jax.ShapeDtypeStruct(water_vel.shape, jnp.float32),
        ),
        in_specs=[vmem] * len(operands),
        out_specs=(vmem, vmem),
        scratch_shapes=[
            pltpu.VMEM((others,) + x.shape, x.dtype) for x in operands[:6]
        ] + [
            pltpu.VMEM((n, con_rows, LANES), jnp.int32),
            pltpu.VMEM((n, con_rows, LANES), jnp.int32),
            pltpu.VMEM((n, 6, con_rows, LANES), jnp.float32),
            pltpu.VMEM((n, half, atom_rows, LANES), jnp.bfloat16),
            pltpu.VMEM((n, LANES, half * LANES), jnp.bfloat16),
            pltpu.VMEM((n, 6 * atom_rows, half * LANES), jnp.bfloat16),
            pltpu.VMEM((n, 3, atom_rows, LANES), jnp.float32),
            pltpu.VMEM((2 * water_pos.shape[0], water_pos.shape[1] // LANES, LANES), jnp.float32),
            pltpu.SemaphoreType.DMA((others, 6)),
            pltpu.SemaphoreType.DMA((others, 6)),
        ],
        compiler_params=pltpu.CompilerParams(
            collective_id=0, has_side_effects=True, vmem_limit_bytes=60 * 1024 * 1024
        ),
    )(*operands)


def solution(mesh):
    in_specs = (
        P(None, ("rep", "dom")),
        P(None, ("rep", "dom")),
        P(("rep", "dom")),
        P(None, ("rep", "dom")),
        P(("rep", "dom")),
        P(("rep", "dom")),
        P(None, ("rep", "dom")),
        P(None, ("rep", "dom")),
    )
    out_specs = (P(None, ("rep", "dom")), P(None, ("rep", "dom")))
    return jax.shard_map(
        functools.partial(on_device, mesh.shape["dom"]),
        mesh=mesh, in_specs=in_specs, out_specs=out_specs, check_vma=False,
    )
```

profile of v0, /device:TPU:9, one launch (start us, length us, event | category | flops | bytes accessed | tf_op | source)
XLA Modules:
  0.0 22.7 jit_solution(15454776100936298994)
XLA Ops:
  0.6 20.0 %shard_map.95 = (f32[3,2048]{1,0:T(4,128)}, f32[9,1024]{1,0:T(8,128)}) custom-call(f32[3,2048]{1,0:T(4,128)} %pos.1, f32[3,2048]{1,0:T(4,128)} %vel.1, f32[16,128]{1,0:T(8,128)} %bitcast.3, s32[2,1280]{1,0:T(2,128)} %bonds.1, s32[3,128]{1,0:T(4,128)} %bitcast.4, s32[3,128]{1,0:T(4,128)} %bitcast.5, f32[9,1024]{1,0:T(8,128)} %wpos.1, f32[9,1024]{1,0:T(8,128)} %wvel.1), custom_call_target="tpu_custom_call" | custom-call | tf_op jit(solution)/shard_map/pallas_call | solution.py:413
  20.6 0.0 copy-start
  20.6 1.4 %copy.12 = f32[3,2048]{1,0:T(4,128)} copy(f32[3,2048]{1,0:T(4,128)} %get-tuple-element.4) | data formatting | bytes 49152
  22.1 0.0 copy-done
  22.1 0.6 %copy.13 = f32[9,1024]{1,0:T(8,128)} copy(f32[9,1024]{1,0:T(8,128)S(1)} %copy-done) | data formatting | bytes 73728
Async XLA Ops:
  20.6 1.4 %copy-start = (f32[9,1024]{1,0:T(8,128)S(1)}, f32[9,1024]{1,0:T(8,128)}, u32[]{:S(2)}) copy-start(f32[9,1024]{1,0:T(8,128)} %get-tuple-element.5) | copy-start | bytes 110596
where the time goes:
time: 22.9 us; the launch traced here: 22.7 us
  Pallas kernels  20 us (87%)
  local copies, waits for them, and re-layouts  2.04 us (9%)
  between operations  0.65 us (3%)
    pallas_call x1, Pallas kernels, on_device(): pl.pallas_call(functools.partial(kernel, n, 'dom'), out_shape=(jax.ShapeD...  20 us
    unnamed x4, local copies, waits for them, and re-layouts  2.04 us

commit v1 on v0

v1 whole, which is shorter than its diff:
```python
import functools
import math

import jax
import jax.numpy as jnp
from jax import lax
from jax.experimental import pallas as pl
from jax.experimental.pallas import tpu as pltpu
from jax.sharding import PartitionSpec as P

ORDER = 4
ITER = 2
LANES = 128
SUB = 8
WIDE = 2 * LANES
F8 = jnp.float8_e4m3fn


time_step = 0.002
mass_oxygen = 15.9994
mass_hydrogen = 1.008
oxygen_hydrogen = 0.09572
hydrogen_pair = 0.15139
total_mass = mass_oxygen + 2.0 * mass_hydrogen
half_pair = 0.5 * hydrogen_pair
water_height = math.sqrt(oxygen_hydrogen * oxygen_hydrogen - half_pair * half_pair)
oxygen_reach = 2.0 * mass_hydrogen * water_height / total_mass
hydrogen_reach = water_height - oxygen_reach


def cross_product(left, right):
    return [
        left[1] * right[2] - left[2] * right[1],
        left[2] * right[0] - left[0] * right[2],
        left[0] * right[1] - left[1] * right[0],
    ]


def inner(left, right):
    return left[0] * right[0] + left[1] * right[1] + left[2] * right[2]


def minus(left, right):
    return [a - b for a, b in zip(left, right)]


def settle(before, after):
    old_oxygen, old_first, old_second = (before[0:3], before[3:6], before[6:9])
    new_oxygen, new_first, new_second = (after[0:3], after[3:6], after[6:9])
    center = [
        (mass_oxygen * o + mass_hydrogen * (f + s)) / total_mass
        for o, f, s in zip(new_oxygen, new_first, new_second)
    ]
    old_b = minus(old_first, old_oxygen)
    old_c = minus(old_second, old_oxygen)
    rel_a = minus(new_oxygen, center)
    rel_b = minus(new_first, center)
    rel_c = minus(new_second, center)
    normal = cross_product(old_b, old_c)
    side = cross_product(rel_a, normal)
    upward = cross_product(normal, side)

    def normed(vector):
        size = jnp.sqrt(inner(vector, vector))
        return [a / size for a in vector]

    axis_z = normed(normal)
    axis_x = normed(side)
    axis_y = normed(upward)
    oldb_x = inner(axis_x, old_b)
    oldb_y = inner(axis_y, old_b)
    oldc_x = inner(axis_x, old_c)
    oldc_y = inner(axis_y, old_c)
    newa_z = inner(axis_z, rel_a)
    newb_x = inner(axis_x, rel_b)
    newb_y = inner(axis_y, rel_b)
    newb_z = inner(axis_z, rel_b)
    newc_x = inner(axis_x, rel_c)
    newc_y = inner(axis_y, rel_c)
    newc_z = inner(axis_z, rel_c)
    sin_phi = newa_z / oxygen_reach
    cos_phi = jnp.sqrt(1.0 - sin_phi * sin_phi)
    sin_psi = (newb_z - newc_z) / (2.0 * half_pair * cos_phi)
    cos_psi = jnp.sqrt(1.0 - sin_psi * sin_psi)
    rest_ay = oxygen_reach * cos_phi
    rest_bx = -half_pair * cos_psi
    lowered = -hydrogen_reach * cos_phi
    tilted = half_pair * sin_psi * sin_phi
    rest_by = lowered - tilted
    rest_cy = lowered + tilted
    alpha = rest_bx * (oldb_x - oldc_x) + oldb_y * rest_by + oldc_y * rest_cy
    beta = rest_bx * (oldc_y - oldb_y) + oldb_x * rest_by + oldc_x * rest_cy
    gamma = oldb_x * newb_y - newb_x * oldb_y + oldc_x * newc_y - newc_x * oldc_y
    summed = alpha * alpha + beta * beta
    sin_theta = (alpha * gamma - beta * jnp.sqrt(summed - gamma * gamma)) / summed
    cos_theta = jnp.sqrt(1.0 - sin_theta * sin_theta)
    final_ax = -rest_ay * sin_theta
    final_ay = rest_ay * cos_theta
    final_bx = rest_bx * cos_theta - rest_by * sin_theta
    final_by = rest_bx * sin_theta + rest_by * cos_theta
    final_cx = -rest_bx * cos_theta - rest_cy * sin_theta
    final_cy = -rest_bx * sin_theta + rest_cy * cos_theta

    def placed(x, y, z):
        return [
            center[c] + axis_x[c] * x + axis_y[c] * y + axis_z[c] * z for c in range(3)
        ]

    return (
        placed(final_ax, final_ay, newa_z)
        + placed(final_bx, final_by, newb_z)
        + placed(final_cx, final_cy, newc_z)
    )


def rounded(x):
    return x.astype(jnp.bfloat16).astype(jnp.float32)


def limbs(x, count):
    parts = []
    for _ in range(count - 1):
        part = rounded(x)
        parts.append(part)
        x = x - part
    return parts + [x]


def dot(a, b):
    return lax.dot_general(
        a, b, (((1,), (0,)), ((), ())), preferred_element_type=jnp.float32
    )


def row_sum(x):
    return jnp.sum(x, axis=0, keepdims=True)


def kernel(
    n, axis, pos, vel, mass, bonds, left, right, wpos, wvel, out_p, out_w,
    pos_x, vel_x, mass_x, bonds_x, left_x, right_x,
    index_s, table_s, scatter_s, gather_s, weight_s, hot_s,
    size_s, scale_s, gap_s, rhs_s, total_s, water_s,
    send_sem, recv_sem,
):
    atoms = pos.shape[1]
    lanes = atoms // SUB
    shift = lanes.bit_length() - 1
    bond_rows = bonds.shape[1] // LANES
    halo_rows = left.shape[0]
    rows = bond_rows + halo_rows
    water_rows = wpos.shape[1] // LANES

    own = (pos, vel, mass, bonds, left, right)
    others = (pos_x, vel_x, mass_x, bonds_x, left_x, right_x)
    me = lax.axis_index(axis)
    copies = []
    if n > 1:
        barrier = pltpu.get_barrier_semaphore()
        for k in range(1, n):
            peer = lax.rem(me + k, n)
            pl.semaphore_signal(
                barrier, inc=1, device_id={axis: peer},
                device_id_type=pl.DeviceIdType.MESH,
            )
        pl.semaphore_wait(barrier, n - 1)
        for k in range(1, n):
            peer = lax.rem(me + n - k, n)
            for t in range(len(own)):
                copy = pltpu.make_async_remote_copy(
                    src_ref=own[t],
                    dst_ref=others[t].at[k - 1],
                    send_sem=send_sem.at[k - 1, t],
                    recv_sem=recv_sem.at[k - 1, t],
                    device_id={axis: peer},
                    device_id_type=pl.DeviceIdType.MESH,
                )
                copy.start()
                copies.append(copy)

    components = wpos.shape[0]
    for source, base in ((wpos, 0), (wvel, components)):
        for c in range(components):
            for r in range(water_rows):
                water_s[base + c, pl.ds(r, 1), :] = source[
                    pl.ds(c, 1), pl.ds(r * LANES, LANES)
                ]
    before = [water_s[c] for c in range(components)]
    speed = [water_s[components + c] for c in range(components)]
    after = [b + time_step * v for b, v in zip(before, speed)]
    settled = settle(before, after)
    for c in range(components):
        water_s[c] = speed[c] + (settled[c] - after[c]) / time_step
    for c in range(components):
        for r in range(water_rows):
            out_w[pl.ds(c, 1), pl.ds(r * LANES, LANES)] = water_s[c, pl.ds(r, 1), :]

    def data(k):
        return own if k == 0 else tuple(ref.at[k - 1] for ref in others)

    def masses(k):
        ref = data(k)[2]
        step = lanes // LANES
        return jnp.concatenate(
            [ref[pl.ds(h, SUB, stride=step), :] for h in range(step)], axis=1
        )

    def index_bonds(k):
        ref = data(k)[3]
        for r in range(bond_rows):
            for e in range(2):
                index_s[k, pl.ds(2 * r + e, 1), :] = ref[
                    pl.ds(e, 1), pl.ds(r * LANES, LANES)
                ]

    def index_cross(k):
        for r in range(halo_rows):
            for e, ref in ((0, data(k)[5]), (1, data(k)[4])):
                index_s[k, pl.ds(2 * (bond_rows + r) + e, 1), :] = ref[pl.ds(r, 1), :]

    def one_hots(k):
        lane = (index_s[k] & (lanes - 1)).astype(jnp.float32)
        turned = lane.T.astype(jnp.bfloat16)
        along = lax.broadcasted_iota(jnp.int32, (LANES, LANES), 1).astype(jnp.float32)
        along = along.astype(jnp.bfloat16)
        down = lax.broadcasted_iota(jnp.int32, (lanes, LANES), 0).astype(jnp.float32)
        down = down.astype(jnp.bfloat16)
        one, zero = jnp.bfloat16(1.0), jnp.bfloat16(0.0)
        for h in range(2 * rows):
            flat = jnp.broadcast_to(lane[h:h + 1], (lanes, LANES)).astype(jnp.bfloat16)
            gather_s[k, :, pl.ds(h * LANES, LANES)] = jnp.where(
                down == flat, one, zero
            ).astype(F8)
            tall = jnp.broadcast_to(turned[:, h:h + 1], (LANES, LANES))
            for q in range(lanes // LANES):
                scatter_s[k, pl.ds(h * LANES, LANES), pl.ds(q * LANES, LANES)] = (
                    jnp.where(along + jnp.bfloat16(q * LANES) == tall, one, zero).astype(F8)
                )

    sub_iota = lax.broadcasted_iota(jnp.int32, (SUB, LANES), 0)

    def hot(k, r, e):
        index = index_s[k, pl.ds(2 * r + e, 1), :]
        return sub_iota == (index >> shift)

    def tables(k):
        position, velocity = data(k)[0], data(k)[1]
        for t, ref in ((0, position), (3, velocity)):
            for c in range(3):
                for r in range(SUB):
                    for q in range(lanes // LANES):
                        table_s[k, pl.ds((t + c) * SUB + r, 1), pl.ds(q * LANES, LANES)] = ref[
                            pl.ds(c, 1), pl.ds(r * lanes + q * LANES, LANES)
                        ]
        place = limbs(table_s[k, pl.ds(0, 3 * SUB), :], 3)
        speed = limbs(table_s[k, pl.ds(3 * SUB, 3 * SUB), :], 2)
        inverse = limbs(masses(k), 2)
        return jnp.concatenate(place + speed + inverse, axis=0)

    def ends(k, stacked, r):
        out = dot(stacked, gather_s[k, :, pl.ds(r * WIDE, WIDE)])

        def take(first, count):
            step = 3 * SUB if first < 15 * SUB else SUB
            total = out[first:first + step]
            for t in range(1, count):
                total = total + out[first + t * step:first + (t + 1) * step]
            return total

        place, speed, inverse = take(0, 3), take(9 * SUB, 2), take(15 * SUB, 2)
        pieces = [place[c * SUB:(c + 1) * SUB] for c in range(3)]
        pieces += [speed[c * SUB:(c + 1) * SUB] for c in range(3)] + [inverse]
        found = []
        for e in range(2):
            mask = hot(k, r, e)
            found.append(
                [jnp.where(mask, p[:, e * LANES:(e + 1) * LANES], 0.0) for p in pieces]
            )
        return found

    def start(k, r, at_i, at_j):
        diff = [row_sum(a - b) for a, b in zip(at_i[0:3], at_j[0:3])]
        rate = [row_sum(a - b) for a, b in zip(at_i[3:6], at_j[3:6])]
        size = jnp.sqrt(inner(diff, diff))
        unit = [d / size for d in diff]
        scale = 1.0 / jnp.sqrt(row_sum(at_i[6] + at_j[6]))
        gap = [d + time_step * v for d, v in zip(diff, rate)]
        size_s[k, pl.ds(r, 1), :] = size
        scale_s[k, pl.ds(r, 1), :] = scale
        for c in range(3):
            gap_s[k, c, pl.ds(r, 1), :] = gap[c]
        rhs_s[k, pl.ds(r, 1), :] = scale * (inner(unit, gap) - size)
        where = (k, k if r < bond_rows else (k + 1) % n)
        for e, sign in ((0, 1.0), (1, -1.0)):
            signed = jnp.where(hot(where[e], r, e), sign, 0.0)
            hot_s[where[e], r, e] = signed
            for c in range(3):
                weight_s[where[e], r, e, c] = signed * (scale * unit[c])

    for copy in copies:
        copy.wait()
    for k in range(n):
        index_bonds(k)
        index_cross(k)
        one_hots(k)
    cross = {}
    for k in range(n):
        stacked = tables(k)
        for r in range(rows):
            at_i, at_j = ends(k, stacked, r)
            if r < bond_rows:
                start(k, r, at_i, at_j)
            else:
                cross[k, r, 0] = at_i
                cross[(k + n - 1) % n, r, 1] = at_j
    for k in range(n):
        for r in range(bond_rows, rows):
            start(k, r, cross[k, r, 0], cross[k, r, 1])

    every = [(k, r) for k in range(n) for r in range(rows)]

    def constraint(k, r, e):
        return (k, r) if e == 0 or r < bond_rows else ((k + n - 1) % n, r)

    def scatter(k, x):
        chains = [None, None]
        for r in range(rows):
            columns = []
            for e in range(2):
                value = x[constraint(k, r, e)]
                high = [value * weight_s[k, r, e, c] for c in range(3)]
                low = [h - rounded(h) for h in high]
                columns.append(jnp.concatenate(high + low, axis=0))
            part = dot(
                jnp.concatenate(columns, axis=1), scatter_s[k, pl.ds(r * WIDE, WIDE), :]
            )
            chains[r % 2] = part if chains[r % 2] is None else chains[r % 2] + part
        summed = chains[0] + chains[1]
        weight = masses(k)
        return [
            weight * (summed[c * SUB:(c + 1) * SUB] + summed[(3 + c) * SUB:(4 + c) * SUB])
            for c in range(3)
        ]

    def gather(k, field):
        stacked = jnp.concatenate(field + [f - rounded(f) for f in field], axis=0)
        found = []
        for r in range(rows):
            out = dot(stacked, gather_s[k, :, pl.ds(r * WIDE, WIDE)])
            both = out[:3 * SUB] + out[3 * SUB:]
            found.append([
                [both[c * SUB:(c + 1) * SUB, e * LANES:(e + 1) * LANES] for c in range(3)]
                for e in range(2)
            ])
        return found

    def at_constraints(found, function):
        partial = {}
        for k in range(n):
            for r in range(rows):
                for e in range(2):
                    partial[constraint(k, r, e) + (e,)] = function(k, r, e, found[k][r][e])
        return partial

    def apply(rhs, x):
        fields = [scatter(k, x) for k in range(n)]
        found = [gather(k, fields[k]) for k in range(n)]
        parts = at_constraints(
            found,
            lambda k, r, e, f: inner([weight_s[k, r, e, c] for c in range(3)], f),
        )
        return {
            (k, r): rhs[k, r] + x[k, r] - row_sum(parts[k, r, 0] + parts[k, r, 1])
            for k, r in every
        }

    def expand(rhs):
        if n > 2:
            return lax.fori_loop(0, ORDER, lambda _, x: apply(rhs, x), rhs)
        x = rhs
        for _ in range(ORDER):
            x = apply(rhs, x)
        return x

    def load_rhs():
        return {(k, r): rhs_s[k, pl.ds(r, 1), :] for k, r in every}

    for c in range(3):
        total_s[c] = jnp.zeros((SUB, lanes), jnp.float32)

    def one_round(_, carry):
        x = expand(load_rhs())
        fields = [scatter(k, x) for k in range(n)]
        for c in range(3):
            total_s[c] = total_s[c] + fields[0][c]
        found = [gather(k, fields[k]) for k in range(n)]
        parts = at_constraints(
            found, lambda k, r, e, f: [hot_s[k, r, e] * f[c] for c in range(3)]
        )
        for k, r in every:
            gap = []
            for c in range(3):
                moved = row_sum(parts[k, r, 0][c] + parts[k, r, 1][c])
                gap.append(gap_s[k, c, pl.ds(r, 1), :] - moved)
                gap_s[k, c, pl.ds(r, 1), :] = gap[c]
            size = size_s[k, pl.ds(r, 1), :]
            scale = scale_s[k, pl.ds(r, 1), :]
            rhs_s[k, pl.ds(r, 1), :] = scale * (
                size - jnp.sqrt(2.0 * size * size - inner(gap, gap))
            )
        return carry

    lax.fori_loop(0, ITER, one_round, 0)
    last = scatter(0, expand(load_rhs()))
    for c in range(3):
        total_s[c] = (total_s[c] + last[c]) / time_step
    for c in range(3):
        for r in range(SUB):
            for q in range(lanes // LANES):
                cols = pl.ds(r * lanes + q * LANES, LANES)
                out_p[pl.ds(c, 1), cols] = (
                    vel[pl.ds(c, 1), cols]
                    - total_s[c, pl.ds(r, 1), pl.ds(q * LANES, LANES)]
                )


def on_device(
    n, protein_pos, protein_vel, inv_mass, bond_atoms, left_atoms, right_atoms, water_pos, water_vel
):
    atoms = protein_pos.shape[1]
    lanes = atoms // SUB
    halo_rows = left_atoms.shape[0] // LANES
    rows = bond_atoms.shape[1] // LANES + halo_rows
    packed = -(-rows // SUB) * SUB
    ends = -(-2 * rows // SUB) * SUB
    others = max(n - 1, 1)
    mass = inv_mass.reshape(atoms // LANES, LANES)
    left = left_atoms.reshape(halo_rows, LANES)
    right = right_atoms.reshape(halo_rows, LANES)
    operands = (protein_pos, protein_vel, mass, bond_atoms, left, right, water_pos, water_vel)
    vmem = pl.BlockSpec(memory_space=pltpu.VMEM)
    return pl.pallas_call(
        functools.partial(kernel, n, "dom"),
        out_shape=(
            jax.ShapeDtypeStruct(protein_vel.shape, jnp.float32),
            jax.ShapeDtypeStruct(water_vel.shape, jnp.float32),
        ),
        in_specs=[vmem] * len(operands),
        out_specs=(vmem, vmem),
        scratch_shapes=[
            pltpu.VMEM((others,) + x.shape, x.dtype) for x in operands[:6]
        ] + [
            pltpu.VMEM((n, ends, LANES), jnp.int32),
            pltpu.VMEM((n, 6 * SUB, lanes), jnp.float32),
            pltpu.VMEM((n, rows * WIDE, lanes), F8),
            pltpu.VMEM((n, lanes, rows * WIDE), F8),
            pltpu.VMEM((n, rows, 2, 3, SUB, LANES), jnp.float32),
            pltpu.VMEM((n, rows, 2, SUB, LANES), jnp.float32),
            pltpu.VMEM((n, packed, LANES), jnp.float32),
            pltpu.VMEM((n, packed, LANES), jnp.float32),
            pltpu.VMEM((n, 3, packed, LANES), jnp.float32),
            pltpu.VMEM((n, packed, LANES), jnp.float32),
            pltpu.VMEM((3, SUB, lanes), jnp.float32),
            pltpu.VMEM((2 * water_pos.shape[0], water_pos.shape[1] // LANES, LANES), jnp.float32),
            pltpu.SemaphoreType.DMA((others, 6)),
            pltpu.SemaphoreType.DMA((others, 6)),
        ],
        compiler_params=pltpu.CompilerParams(
            collective_id=0, has_side_effects=True, vmem_limit_bytes=60 * 1024 * 1024
        ),
    )(*operands)


def solution(mesh):
    in_specs = (
        P(None, ("rep", "dom")),
        P(None, ("rep", "dom")),
        P(("rep", "dom")),
        P(None, ("rep", "dom")),
        P(("rep", "dom")),
        P(("rep", "dom")),
        P(None, ("rep", "dom")),
        P(None, ("rep", "dom")),
    )
    out_specs = (P(None, ("rep", "dom")), P(None, ("rep", "dom")))
    return jax.shard_map(
        functools.partial(on_device, mesh.shape["dom"]),
        mesh=mesh, in_specs=in_specs, out_specs=out_specs, check_vma=False,
    )
```

time: 22.9 us -> 16.8 us (0.73)
  Pallas kernels: 20 us -> 13.9 us
    pallas_call x1, Pallas kernels: 20 us -> 13.9 us  [on_device(): pl.pallas_call(functools.partial(kernel, n, 'dom'), out_shape=(jax.ShapeD...]
where the time goes in v1:
time: 16.8 us; the launch traced here: 16.6 us
  Pallas kernels  13.9 us (83%)
  local copies, waits for them, and re-layouts  2.04 us (12%)
  between operations  0.65 us (4%)
    pallas_call x1, Pallas kernels, on_device(): pl.pallas_call(functools.partial(kernel, n, 'dom'), out_shape=(jax.ShapeD...  13.9 us
    unnamed x4, local copies, waits for them, and re-layouts  2.04 us

profile of v1, /device:TPU:9, one launch (start us, length us, event | category | flops | bytes accessed | tf_op | source)
XLA Modules:
  0.0 16.6 jit_solution(16907911244399551750)
XLA Ops:
  0.6 13.9 %shard_map.95 = (f32[3,2048]{1,0:T(4,128)}, f32[9,1024]{1,0:T(8,128)}) custom-call(f32[3,2048]{1,0:T(4,128)} %pos.1, f32[3,2048]{1,0:T(4,128)} %vel.1, f32[16,128]{1,0:T(8,128)} %bitcast.3, s32[2,1280]{1,0:T(2,128)} %bonds.1, s32[3,128]{1,0:T(4,128)} %bitcast.4, s32[3,128]{1,0:T(4,128)} %bitcast.5, f32[9,1024]{1,0:T(8,128)} %wpos.1, f32[9,1024]{1,0:T(8,128)} %wvel.1), custom_call_target="tpu_custom_call" | custom-call | tf_op jit(solution)/shard_map/pallas_call | solution.py:442
  14.5 0.0 copy-start
  14.5 1.4 %copy.12 = f32[3,2048]{1,0:T(4,128)} copy(f32[3,2048]{1,0:T(4,128)} %get-tuple-element.4) | data formatting | bytes 49152
  15.9 0.0 copy-done
  16.0 0.6 %copy.13 = f32[9,1024]{1,0:T(8,128)} copy(f32[9,1024]{1,0:T(8,128)S(1)} %copy-done) | data formatting | bytes 73728
Async XLA Ops:
  14.5 1.4 %copy-start = (f32[9,1024]{1,0:T(8,128)S(1)}, f32[9,1024]{1,0:T(8,128)}, u32[]{:S(2)}) copy-start(f32[9,1024]{1,0:T(8,128)} %get-tuple-element.5) | copy-start | bytes 110596

commit v2 on v1

--- a/solution.py
+++ b/solution.py
@@ -137,12 +137,17 @@
 
 
 def kernel(
-    n, axis, pos, vel, mass, bonds, left, right, wpos, wvel, out_p, out_w,
-    pos_x, vel_x, mass_x, bonds_x, left_x, right_x,
+    n, axis, *refs
+):
+    given, refs = refs[:8], refs[8:]
+    out_p, out_w = refs[:2]
+    pos, vel, mass, bonds, left, right, wpos, wvel = refs[2:10]
+    pos_x, vel_x, mass_x, bonds_x, left_x, right_x = refs[10:16]
+    (
     index_s, table_s, scatter_s, gather_s, weight_s, hot_s,
     size_s, scale_s, gap_s, rhs_s, total_s, water_s,
-    send_sem, recv_sem,
-):
+    load_sem, send_sem, recv_sem,
+    ) = refs[16:]
     atoms = pos.shape[1]
     lanes = atoms // SUB
     shift = lanes.bit_length() - 1
@@ -154,6 +159,12 @@
     own = (pos, vel, mass, bonds, left, right)
     others = (pos_x, vel_x, mass_x, bonds_x, left_x, right_x)
     me = lax.axis_index(axis)
+    loads = [
+        pltpu.make_async_copy(source, to, load_sem.at[t])
+        for t, (source, to) in enumerate(zip(given, own + (wpos, wvel)))
+    ]
+    for load in loads:
+        load.start()
     copies = []
     if n > 1:
         barrier = pltpu.get_barrier_semaphore()
@@ -163,6 +174,9 @@
                 barrier, inc=1, device_id={axis: peer},
                 device_id_type=pl.DeviceIdType.MESH,
             )
+    for load in loads[:len(own)]:
+        load.wait()
+    if n > 1:
         pl.semaphore_wait(barrier, n - 1)
         for k in range(1, n):
             peer = lax.rem(me + n - k, n)
@@ -178,6 +192,8 @@
                 copy.start()
                 copies.append(copy)
 
+    for load in loads[len(own):]:
+        load.wait()
     components = wpos.shape[0]
     for source, base in ((wpos, 0), (wvel, components)):
         for c in range(components):
@@ -297,14 +313,12 @@
             for c in range(3):
                 weight_s[where[e], r, e, c] = signed * (scale * unit[c])
 
-    for copy in copies:
-        copy.wait()
-    for k in range(n):
+    cross = {}
+
+    def prepare(k):
         index_bonds(k)
         index_cross(k)
         one_hots(k)
-    cross = {}
-    for k in range(n):
         stacked = tables(k)
         for r in range(rows):
             at_i, at_j = ends(k, stacked, r)
@@ -313,6 +327,12 @@
             else:
                 cross[k, r, 0] = at_i
                 cross[(k + n - 1) % n, r, 1] = at_j
+
+    prepare(0)
+    for copy in copies:
+        copy.wait()
+    for k in range(1, n):
+        prepare(k)
     for k in range(n):
         for r in range(bond_rows, rows):
             start(k, r, cross[k, r, 0], cross[k, r, 1])
@@ -335,12 +355,15 @@
                 jnp.concatenate(columns, axis=1), scatter_s[k, pl.ds(r * WIDE, WIDE), :]
             )
             chains[r % 2] = part if chains[r % 2] is None else chains[r % 2] + part
-        summed = chains[0] + chains[1]
         weight = masses(k)
-        return [
-            weight * (summed[c * SUB:(c + 1) * SUB] + summed[(3 + c) * SUB:(4 + c) * SUB])
-            for c in range(3)
+        pieces = [
+            [
+                weight * (p[c * SUB:(c + 1) * SUB] + p[(3 + c) * SUB:(4 + c) * SUB])
+                for c in range(3)
+            ]
+            for p in chains
         ]
+        return [a + b for a, b in zip(*pieces)]
 
     def gather(k, field):
         stacked = jnp.concatenate(field + [f - rounded(f) for f in field], axis=0)
@@ -424,6 +447,11 @@
                 )
 
 
+def hand_over(p, w, out_p, out_w):
+    out_p[...] = p[...]
+    out_w[...] = w[...]
+
+
 def on_device(
     n, protein_pos, protein_vel, inv_mass, bond_atoms, left_atoms, right_atoms, water_pos, water_vel
 ):
@@ -439,15 +467,15 @@
     right = right_atoms.reshape(halo_rows, LANES)
     operands = (protein_pos, protein_vel, mass, bond_atoms, left, right, water_pos, water_vel)
     vmem = pl.BlockSpec(memory_space=pltpu.VMEM)
-    return pl.pallas_call(
+    results = pl.pallas_call(
         functools.partial(kernel, n, "dom"),
         out_shape=(
-            jax.ShapeDtypeStruct(protein_vel.shape, jnp.float32),
-            jax.ShapeDtypeStruct(water_vel.shape, jnp.float32),
+            pltpu.VMEM(protein_vel.shape, jnp.float32),
+            pltpu.VMEM(water_vel.shape, jnp.float32),
         ),
-        in_specs=[vmem] * len(operands),
+        in_specs=[pl.BlockSpec(memory_space=pltpu.HBM)] * len(operands),
         out_specs=(vmem, vmem),
-        scratch_shapes=[
+        scratch_shapes=[pltpu.VMEM(x.shape, x.dtype) for x in operands] + [
             pltpu.VMEM((others,) + x.shape, x.dtype) for x in operands[:6]
         ] + [
             pltpu.VMEM((n, ends, LANES), jnp.int32),
@@ -462,6 +490,7 @@
             pltpu.VMEM((n, packed, LANES), jnp.float32),
             pltpu.VMEM((3, SUB, lanes), jnp.float32),
             pltpu.VMEM((2 * water_pos.shape[0], water_pos.shape[1] // LANES, LANES), jnp.float32),
+            pltpu.SemaphoreType.DMA((len(operands),)),
             pltpu.SemaphoreType.DMA((others, 6)),
             pltpu.SemaphoreType.DMA((others, 6)),
         ],
@@ -469,6 +498,13 @@
             collective_id=0, has_side_effects=True, vmem_limit_bytes=60 * 1024 * 1024
         ),
     )(*operands)
+    return pl.pallas_call(
+        hand_over,
+        out_shape=[jax.ShapeDtypeStruct(x.shape, x.dtype) for x in results],
+        in_specs=[vmem] * 2,
+        out_specs=[vmem] * 2,
+        compiler_params=pltpu.CompilerParams(vmem_limit_bytes=8 * 1024 * 1024),
+    )(*results)
 
 
 def solution(mesh):

time: 16.8 us -> 12.6 us (0.75)
  Pallas kernels: 13.9 us -> 11.7 us
  local copies, waits for them, and re-layouts: 2.04 us -> 0 us
    pallas_call x1 -> x2, Pallas kernels: 13.9 us -> 11.7 us  [the longest x1 11.1 us: on_device(): pl.pallas_call(functools.partial(kernel, n, 'dom'), out_shape=(pltpu.VMEM...]
    unnamed x4 -> x0, local copies, waits for them, and re-layouts: 2.04 us -> none
where the time goes in v2:
time: 12.6 us; the launch traced here: 12.4 us
  Pallas kernels  11.7 us (93%)
  between operations  0.64 us (5%)
    pallas_call x1, Pallas kernels, on_device(): pl.pallas_call(functools.partial(kernel, n, 'dom'), out_shape=(pltpu.VMEM...  11.1 us
    pallas_call x1, Pallas kernels, on_device(): pl.pallas_call(hand_over, out_shape=[jax.ShapeDtypeStruct(x.shape, x.dtyp...  0.65 us

profile of v2, /device:TPU:9, one launch (start us, length us, event | category | flops | bytes accessed | tf_op | source)
XLA Modules:
  0.0 12.4 jit_solution(15054205234957617727)
XLA Ops:
  0.6 11.1 %shard_map.95 = (f32[3,2048]{1,0:T(4,128)S(1)}, f32[9,1024]{1,0:T(8,128)S(1)}) custom-call(f32[3,2048]{1,0:T(4,128)} %refs_0_.1, f32[3,2048]{1,0:T(4,128)} %refs_1_.1, f32[16,128]{1,0:T(8,128)} %bitcast.3, s32[2,1280]{1,0:T(2,128)} %refs_3_.1, s32[3,128]{1,0:T(4,128)} %bitcast.4, s32[3,128]{1,0:T(4,128)} %bitcast.5, f32[9,1024]{1,0:T(8,128)} %refs_6_.1, ...), custom_call_target="tpu_custom_call" | custom-call | tf_op jit(solution)/shard_map/pallas_call | solution.py:470
  11.7 0.6 %shard_map.96 = (f32[3,2048]{1,0:T(4,128)}, f32[9,1024]{1,0:T(8,128)}) custom-call(f32[3,2048]{1,0:T(4,128)S(1)} %get-tuple-element.4.p, f32[9,1024]{1,0:T(8,128)S(1)} %get-tuple-element.5.w), custom_call_target="tpu_custom_call" | custom-call | tf_op jit(solution)/shard_map/pallas_call | solution.py:501

commit v3 on v2

--- a/solution.py
+++ b/solution.py
@@ -349,7 +349,7 @@
             for e in range(2):
                 value = x[constraint(k, r, e)]
                 high = [value * weight_s[k, r, e, c] for c in range(3)]
-                low = [h - rounded(h) for h in high]
+                low = [rounded(h) - h for h in high]
                 columns.append(jnp.concatenate(high + low, axis=0))
             part = dot(
                 jnp.concatenate(columns, axis=1), scatter_s[k, pl.ds(r * WIDE, WIDE), :]
@@ -358,7 +358,7 @@
         weight = masses(k)
         pieces = [
             [
-                weight * (p[c * SUB:(c + 1) * SUB] + p[(3 + c) * SUB:(4 + c) * SUB])
+                weight * (p[c * SUB:(c + 1) * SUB] - p[(3 + c) * SUB:(4 + c) * SUB])
                 for c in range(3)
             ]
             for p in chains
@@ -366,11 +366,11 @@
         return [a + b for a, b in zip(*pieces)]
 
     def gather(k, field):
-        stacked = jnp.concatenate(field + [f - rounded(f) for f in field], axis=0)
+        stacked = jnp.concatenate(field + [rounded(f) - f for f in field], axis=0)
         found = []
         for r in range(rows):
             out = dot(stacked, gather_s[k, :, pl.ds(r * WIDE, WIDE)])
-            both = out[:3 * SUB] + out[3 * SUB:]
+            both = out[:3 * SUB] - out[3 * SUB:]
             found.append([
                 [both[c * SUB:(c + 1) * SUB, e * LANES:(e + 1) * LANES] for c in range(3)]
                 for e in range(2)
@@ -433,7 +433,11 @@
             )
         return carry
 
-    lax.fori_loop(0, ITER, one_round, 0)
+    if n > 2:
+        lax.fori_loop(0, ITER, one_round, 0)
+    else:
+        for _ in range(ITER):
+            one_round(0, 0)
     last = scatter(0, expand(load_rhs()))
     for c in range(3):
         total_s[c] = (total_s[c] + last[c]) / time_step

time: 12.6 us -> 11.5 us (0.913)
  Pallas kernels: 11.7 us -> 10.7 us
    pallas_call x1, Pallas kernels: 11.1 us -> 10 us  [on_device(): pl.pallas_call(functools.partial(kernel, n, 'dom'), out_shape=(pltpu.VMEM...]
where the time goes in v3:
time: 11.5 us; the launch traced here: 11.3 us
  Pallas kernels  10.7 us (93%)
  between operations  0.64 us (6%)
    pallas_call x1, Pallas kernels, on_device(): pl.pallas_call(functools.partial(kernel, n, 'dom'), out_shape=(pltpu.VMEM...  10 us
    pallas_call x1, Pallas kernels, on_device(): pl.pallas_call(hand_over, out_shape=[jax.ShapeDtypeStruct(x.shape, x.dtyp...  0.65 us

profile of v3, /device:TPU:9, one launch (start us, length us, event | category | flops | bytes accessed | tf_op | source)
XLA Modules:
  0.0 11.3 jit_solution(16127950117932025953)
XLA Ops:
  0.6 10.0 %shard_map.95 = (f32[3,2048]{1,0:T(4,128)S(1)}, f32[9,1024]{1,0:T(8,128)S(1)}) custom-call(f32[3,2048]{1,0:T(4,128)} %refs_0_.1, f32[3,2048]{1,0:T(4,128)} %refs_1_.1, f32[16,128]{1,0:T(8,128)} %bitcast.3, s32[2,1280]{1,0:T(2,128)} %refs_3_.1, s32[3,128]{1,0:T(4,128)} %bitcast.4, s32[3,128]{1,0:T(4,128)} %bitcast.5, f32[9,1024]{1,0:T(8,128)} %refs_6_.1, ...), custom_call_target="tpu_custom_call" | custom-call | tf_op jit(solution)/shard_map/pallas_call | solution.py:474
  10.7 0.6 %shard_map.96 = (f32[3,2048]{1,0:T(4,128)}, f32[9,1024]{1,0:T(8,128)}) custom-call(f32[3,2048]{1,0:T(4,128)S(1)} %get-tuple-element.4.p, f32[9,1024]{1,0:T(8,128)S(1)} %get-tuple-element.5.w), custom_call_target="tpu_custom_call" | custom-call | tf_op jit(solution)/shard_map/pallas_call | solution.py:505

commit v4 on v3

--- a/solution.py
+++ b/solution.py
@@ -145,7 +145,7 @@
     pos_x, vel_x, mass_x, bonds_x, left_x, right_x = refs[10:16]
     (
     index_s, table_s, scatter_s, gather_s, weight_s, hot_s,
-    size_s, scale_s, gap_s, rhs_s, total_s, water_s,
+    size_s, scale_s, gap_s, rhs_s, tile_s, field_s, total_s, water_s,
     load_sem, send_sem, recv_sem,
     ) = refs[16:]
     atoms = pos.shape[1]
@@ -154,6 +154,9 @@
     bond_rows = bonds.shape[1] // LANES
     halo_rows = left.shape[0]
     rows = bond_rows + halo_rows
+    pairs = SUB // 2
+    groups = [min(1 if k == 0 else 2, bond_rows // pairs) for k in range(n)]
+    picked = [g * pairs for g in groups]
     water_rows = wpos.shape[1] // LANES
 
     own = (pos, vel, mass, bonds, left, right)
@@ -311,7 +314,12 @@
             signed = jnp.where(hot(where[e], r, e), sign, 0.0)
             hot_s[where[e], r, e] = signed
             for c in range(3):
-                weight_s[where[e], r, e, c] = signed * (scale * unit[c])
+                weight = scale * unit[c]
+                weight_s[where[e], r, e, c] = signed * weight
+                if r < picked[k]:
+                    tile_s[k, r // pairs, c, pl.ds(2 * (r % pairs) + e, 1), :] = (
+                        sign * weight
+                    )
 
     cross = {}
 
@@ -367,8 +375,8 @@
 
     def gather(k, field):
         stacked = jnp.concatenate(field + [rounded(f) - f for f in field], axis=0)
-        found = []
-        for r in range(rows):
+        found = [None] * picked[k]
+        for r in range(picked[k], rows):
             out = dot(stacked, gather_s[k, :, pl.ds(r * WIDE, WIDE)])
             both = out[:3 * SUB] - out[3 * SUB:]
             found.append([
@@ -377,25 +385,62 @@
             ])
         return found
 
+    def pick(k, g):
+        index = index_s[k, pl.ds(g * SUB, SUB), :]
+        lane, block = index & (LANES - 1), index >> (LANES.bit_length() - 1)
+        taken = [None] * 3
+        per_row = lanes // LANES
+        for s in range(SUB):
+            for q in range(per_row):
+                hit = block == s * per_row + q
+                for c in range(3):
+                    source = jnp.broadcast_to(
+                        field_s[k, c, pl.ds(s, 1), pl.ds(q * LANES, LANES)], (SUB, LANES)
+                    )
+                    got = jnp.take_along_axis(
+                        source, lane, axis=1, mode="promise_in_bounds"
+                    )
+                    old = taken[c]
+                    taken[c] = got if old is None else jnp.where(hit, got, old)
+        return taken
+
+    def picks(fields):
+        for k in range(n):
+            for c in range(3):
+                field_s[k, c] = fields[k][c]
+        return [[pick(k, g) for g in range(groups[k])] for k in range(n)]
+
+    def at_even(x, q):
+        return jnp.broadcast_to(x[2 * q:2 * q + 1], (SUB, LANES))
+
     def at_constraints(found, function):
         partial = {}
         for k in range(n):
-            for r in range(rows):
+            for r in range(picked[k], rows):
                 for e in range(2):
                     partial[constraint(k, r, e) + (e,)] = function(k, r, e, found[k][r][e])
         return partial
 
     def apply(rhs, x):
         fields = [scatter(k, x) for k in range(n)]
+        taken = picks(fields)
         found = [gather(k, fields[k]) for k in range(n)]
         parts = at_constraints(
             found,
             lambda k, r, e, f: inner([weight_s[k, r, e, c] for c in range(3)], f),
         )
-        return {
-            (k, r): rhs[k, r] + x[k, r] - row_sum(parts[k, r, 0] + parts[k, r, 1])
-            for k, r in every
-        }
+        near = [
+            [inner([tile_s[k, g, c] for c in range(3)], taken[k][g]) for g in range(groups[k])]
+            for k in range(n)
+        ]
+        near = [[t + pltpu.roll(t, SUB - 1, 0) for t in some] for some in near]
+
+        def change(k, r):
+            if r < picked[k]:
+                return at_even(near[k][r // pairs], r % pairs)
+            return row_sum(parts[k, r, 0] + parts[k, r, 1])
+
+        return {(k, r): rhs[k, r] + x[k, r] - change(k, r) for k, r in every}
 
     def expand(rhs):
         if n > 2:
@@ -406,7 +451,10 @@
         return x
 
     def load_rhs():
-        return {(k, r): rhs_s[k, pl.ds(r, 1), :] for k, r in every}
+        return {
+            (k, r): jnp.broadcast_to(rhs_s[k, pl.ds(r, 1), :], (SUB, LANES))
+            for k, r in every
+        }
 
     for c in range(3):
         total_s[c] = jnp.zeros((SUB, lanes), jnp.float32)
@@ -416,14 +464,23 @@
         fields = [scatter(k, x) for k in range(n)]
         for c in range(3):
             total_s[c] = total_s[c] + fields[0][c]
+        taken = picks(fields)
         found = [gather(k, fields[k]) for k in range(n)]
         parts = at_constraints(
             found, lambda k, r, e, f: [hot_s[k, r, e] * f[c] for c in range(3)]
         )
+        near = [
+            [[t - pltpu.roll(t, SUB - 1, 0) for t in some] for some in taken[k]]
+            for k in range(n)
+        ]
         for k, r in every:
             gap = []
             for c in range(3):
-                moved = row_sum(parts[k, r, 0][c] + parts[k, r, 1][c])
+                if r < picked[k]:
+                    q = 2 * (r % pairs)
+                    moved = near[k][r // pairs][c][q:q + 1]
+                else:
+                    moved = row_sum(parts[k, r, 0][c] + parts[k, r, 1][c])
                 gap.append(gap_s[k, c, pl.ds(r, 1), :] - moved)
                 gap_s[k, c, pl.ds(r, 1), :] = gap[c]
             size = size_s[k, pl.ds(r, 1), :]
@@ -492,6 +549,8 @@
             pltpu.VMEM((n, packed, LANES), jnp.float32),
             pltpu.VMEM((n, 3, packed, LANES), jnp.float32),
             pltpu.VMEM((n, packed, LANES), jnp.float32),
+            pltpu.VMEM((n, rows, 3, SUB, LANES), jnp.float32),
+            pltpu.VMEM((n, 3, SUB, lanes), jnp.float32),
             pltpu.VMEM((3, SUB, lanes), jnp.float32),
             pltpu.VMEM((2 * water_pos.shape[0], water_pos.shape[1] // LANES, LANES), jnp.float32),
             pltpu.SemaphoreType.DMA((len(operands),)),

time: 11.5 us -> 10.7 us (0.930)
  Pallas kernels: 10.7 us -> 9.9 us
    pallas_call x1, Pallas kernels: 10 us -> 9.25 us  [on_device(): pl.pallas_call(functools.partial(kernel, n, 'dom'), out_shape=(pltpu.VMEM...]
where the time goes in v4:
time: 10.7 us; the launch traced here: 10.5 us
  Pallas kernels  9.9 us (93%)
  between operations  0.64 us (6%)
    pallas_call x1, Pallas kernels, on_device(): pl.pallas_call(functools.partial(kernel, n, 'dom'), out_shape=(pltpu.VMEM...  9.25 us
    pallas_call x1, Pallas kernels, on_device(): pl.pallas_call(hand_over, out_shape=[jax.ShapeDtypeStruct(x.shape, x.dtyp...  0.65 us

profile of v4, /device:TPU:9, one launch (start us, length us, event | category | flops | bytes accessed | tf_op | source)
XLA Modules:
  0.0 10.5 jit_solution(13485308377868015854)
XLA Ops:
  0.6 9.3 %shard_map.95 = (f32[3,2048]{1,0:T(4,128)S(1)}, f32[9,1024]{1,0:T(8,128)S(1)}) custom-call(f32[3,2048]{1,0:T(4,128)} %refs_0_.1, f32[3,2048]{1,0:T(4,128)} %refs_1_.1, f32[16,128]{1,0:T(8,128)} %bitcast.3, s32[2,1280]{1,0:T(2,128)} %refs_3_.1, s32[3,128]{1,0:T(4,128)} %bitcast.4, s32[3,128]{1,0:T(4,128)} %bitcast.5, f32[9,1024]{1,0:T(8,128)} %refs_6_.1, ...), custom_call_target="tpu_custom_call" | custom-call | tf_op jit(solution)/shard_map/pallas_call | solution.py:531
  9.9 0.6 %shard_map.96 = (f32[3,2048]{1,0:T(4,128)}, f32[9,1024]{1,0:T(8,128)}) custom-call(f32[3,2048]{1,0:T(4,128)S(1)} %get-tuple-element.4.p, f32[9,1024]{1,0:T(8,128)S(1)} %get-tuple-element.5.w), custom_call_target="tpu_custom_call" | custom-call | tf_op jit(solution)/shard_map/pallas_call | solution.py:564

commit v5 on v4

--- a/solution.py
+++ b/solution.py
@@ -145,7 +145,7 @@
     pos_x, vel_x, mass_x, bonds_x, left_x, right_x = refs[10:16]
     (
     index_s, table_s, scatter_s, gather_s, weight_s, hot_s,
-    size_s, scale_s, gap_s, rhs_s, tile_s, field_s, total_s, water_s,
+    raw_s, size_s, scale_s, gap_s, rhs_s, tile_s, field_s, total_s, water_s,
     load_sem, send_sem, recv_sem,
     ) = refs[16:]
     atoms = pos.shape[1]
@@ -297,28 +297,40 @@
             )
         return found
 
-    def start(k, r, at_i, at_j):
-        diff = [row_sum(a - b) for a, b in zip(at_i[0:3], at_j[0:3])]
-        rate = [row_sum(a - b) for a, b in zip(at_i[3:6], at_j[3:6])]
-        size = jnp.sqrt(inner(diff, diff))
+    def collect(k, r, at_i, at_j):
+        for t in range(6):
+            raw_s[k, t, pl.ds(r, 1), :] = row_sum(at_i[t] - at_j[t])
+        raw_s[k, 6, pl.ds(r, 1), :] = row_sum(at_i[6] + at_j[6])
+
+    def start(k, first, count):
+        span = pl.ds(first, count)
+        shape = (count, LANES)
+        valid = lax.broadcasted_iota(jnp.int32, shape, 0) < rows - first
+        diff = [raw_s[k, c, span, :] for c in range(3)]
+        size = jnp.where(valid, jnp.sqrt(inner(diff, diff)), 1.0)
         unit = [d / size for d in diff]
-        scale = 1.0 / jnp.sqrt(row_sum(at_i[6] + at_j[6]))
-        gap = [d + time_step * v for d, v in zip(diff, rate)]
-        size_s[k, pl.ds(r, 1), :] = size
-        scale_s[k, pl.ds(r, 1), :] = scale
+        scale = jnp.where(valid, 1.0 / jnp.sqrt(raw_s[k, 6, span, :]), 0.0)
+        gap = [d + time_step * raw_s[k, 3 + c, span, :] for c, d in enumerate(diff)]
+        size_s[k, span, :] = size
+        scale_s[k, span, :] = scale
         for c in range(3):
-            gap_s[k, c, pl.ds(r, 1), :] = gap[c]
-        rhs_s[k, pl.ds(r, 1), :] = scale * (inner(unit, gap) - size)
+            gap_s[k, c, span, :] = gap[c]
+            raw_s[k, c, span, :] = scale * unit[c]
+        rhs_s[k, span, :] = scale * (inner(unit, gap) - size)
+        for r in range(first, min(first + count, rows)):
+            weigh(k, r)
+
+    def weigh(k, r):
         where = (k, k if r < bond_rows else (k + 1) % n)
+        weight = [raw_s[k, c, pl.ds(r, 1), :] for c in range(3)]
         for e, sign in ((0, 1.0), (1, -1.0)):
             signed = jnp.where(hot(where[e], r, e), sign, 0.0)
             hot_s[where[e], r, e] = signed
             for c in range(3):
-                weight = scale * unit[c]
-                weight_s[where[e], r, e, c] = signed * weight
+                weight_s[where[e], r, e, c] = signed * weight[c]
                 if r < picked[k]:
                     tile_s[k, r // pairs, c, pl.ds(2 * (r % pairs) + e, 1), :] = (
-                        sign * weight
+                        sign * weight[c]
                     )
 
     cross = {}
@@ -331,19 +343,25 @@
         for r in range(rows):
             at_i, at_j = ends(k, stacked, r)
             if r < bond_rows:
-                start(k, r, at_i, at_j)
+                collect(k, r, at_i, at_j)
             else:
                 cross[k, r, 0] = at_i
                 cross[(k + n - 1) % n, r, 1] = at_j
 
     prepare(0)
+    whole = bond_rows // SUB * SUB
+    if whole:
+        start(0, 0, whole)
     for copy in copies:
         copy.wait()
     for k in range(1, n):
         prepare(k)
     for k in range(n):
         for r in range(bond_rows, rows):
-            start(k, r, cross[k, r, 0], cross[k, r, 1])
+            collect(k, r, cross[k, r, 0], cross[k, r, 1])
+    for k in range(n):
+        first = whole if k == 0 else 0
+        start(k, first, size_s.shape[1] - first)
 
     every = [(k, r) for k in range(n) for r in range(rows)]
 
@@ -362,7 +380,8 @@
             part = dot(
                 jnp.concatenate(columns, axis=1), scatter_s[k, pl.ds(r * WIDE, WIDE), :]
             )
-            chains[r % 2] = part if chains[r % 2] is None else chains[r % 2] + part
+            lot = (r + k) % 2
+            chains[lot] = part if chains[lot] is None else chains[lot] + part
         weight = masses(k)
         pieces = [
             [
@@ -375,14 +394,14 @@
 
     def gather(k, field):
         stacked = jnp.concatenate(field + [rounded(f) - f for f in field], axis=0)
-        found = [None] * picked[k]
-        for r in range(picked[k], rows):
+        found = [None] * rows
+        for r in list(range(bond_rows, rows)) + list(range(picked[k], bond_rows)):
             out = dot(stacked, gather_s[k, :, pl.ds(r * WIDE, WIDE)])
             both = out[:3 * SUB] - out[3 * SUB:]
-            found.append([
+            found[r] = [
                 [both[c * SUB:(c + 1) * SUB, e * LANES:(e + 1) * LANES] for c in range(3)]
                 for e in range(2)
-            ])
+            ]
         return found
 
     def pick(k, g):
@@ -545,6 +564,7 @@
             pltpu.VMEM((n, lanes, rows * WIDE), F8),
             pltpu.VMEM((n, rows, 2, 3, SUB, LANES), jnp.float32),
             pltpu.VMEM((n, rows, 2, SUB, LANES), jnp.float32),
+            pltpu.VMEM((n, 7, packed, LANES), jnp.float32),
             pltpu.VMEM((n, packed, LANES), jnp.float32),
             pltpu.VMEM((n, packed, LANES), jnp.float32),
             pltpu.VMEM((n, 3, packed, LANES), jnp.float32),

time: 10.7 us -> 10.7 us (level)
  no operation moved by 1% of the time
where the time goes in v5:
time: 10.7 us; the launch traced here: 10.5 us
  Pallas kernels  9.89 us (92%)
  between operations  0.64 us (6%)
    pallas_call x1, Pallas kernels, on_device(): pl.pallas_call(functools.partial(kernel, n, 'dom'), out_shape=(pltpu.VMEM...  9.24 us
    pallas_call x1, Pallas kernels, on_device(): pl.pallas_call(hand_over, out_shape=[jax.ShapeDtypeStruct(x.shape, x.dtyp...  0.65 us

profile of v5, /device:TPU:9, one launch (start us, length us, event | category | flops | bytes accessed | tf_op | source)
XLA Modules:
  0.0 10.5 jit_solution(15594616336909620247)
XLA Ops:
  0.6 9.2 %shard_map.95 = (f32[3,2048]{1,0:T(4,128)S(1)}, f32[9,1024]{1,0:T(8,128)S(1)}) custom-call(f32[3,2048]{1,0:T(4,128)} %refs_0_.1, f32[3,2048]{1,0:T(4,128)} %refs_1_.1, f32[16,128]{1,0:T(8,128)} %bitcast.3, s32[2,1280]{1,0:T(2,128)} %refs_3_.1, s32[3,128]{1,0:T(4,128)} %bitcast.4, s32[3,128]{1,0:T(4,128)} %bitcast.5, f32[9,1024]{1,0:T(8,128)} %refs_6_.1, ...), custom_call_target="tpu_custom_call" | custom-call | tf_op jit(solution)/shard_map/pallas_call | solution.py:550
  9.9 0.6 %shard_map.96 = (f32[3,2048]{1,0:T(4,128)}, f32[9,1024]{1,0:T(8,128)}) custom-call(f32[3,2048]{1,0:T(4,128)S(1)} %get-tuple-element.4.p, f32[9,1024]{1,0:T(8,128)S(1)} %get-tuple-element.5.w), custom_call_target="tpu_custom_call" | custom-call | tf_op jit(solution)/shard_map/pallas_call | solution.py:584
